TPU v7x, 32 devices: a whole 2x2x4 slice. The times are simulated.
32 devices in a mesh: vocab: 16 (over z, y, x), dp: 2 (over core).
Axes of the slice: x: 2, y: 2, z: 4, core: 2. Of those that a mesh axis runs over, the one named last changes fastest.
Arguments:
- embed_table: bfloat16 [16384, 4096], P('vocab'), may hold values from -3 to 3
- token_ids: int32 [2, 16384], P('dp', 'vocab'), may hold values from 0 to 16383, as said below
- grad_rows: bfloat16 [2, 16384, 4096], P('dp', 'vocab'), may hold values from -12 to 12
Outputs:
- updated: bfloat16 [16384, 4096], P('vocab', 'dp')
- grad_rms: float32 [1], replicated
Inputs may be any that keep to these rules, and one draw needn't show every extreme that they name: `token_ids`: rows are read cyclically: row r stands for every r + k * 16384. The window of vocab index v (tokens v * 1024 to (v + 1) * 1024 - 1 of a replica) holds ids that, read as the cyclic representatives from v * 1024 - 256 to (v + 1) * 1024 + 255, rise (never fall) along its tokens; both ends are reached in some window. Only its first 128 and last 128 tokens may lie outside rows v * 1024 to (v + 1) * 1024 - 1 (so read), the first ones below, the last ones above; in every window its first token lies below and its last above, in some window all first 128 lie below, in some all last 128 above.
All inputs are finite; a program needn't handle non-finite values.
Results may differ from a plain program's by a relative error of at most 0.002.
Values may be sent and summed in bfloat16 or wider, within the bound.
A program may use at most 128 MiB of HBM per device.

v0:
```python
import jax
import jax.numpy as jnp
from jax import lax
from jax.sharding import PartitionSpec as P

TOK_EDGE = 128


step_rate = 0.5
norm_limit = 1.0


def shifted(block, axis, distance):
    devices = range(lax.axis_size(axis))
    route = [((i - distance) % len(devices), i) for i in devices]
    return lax.ppermute(block, axis, route)


def onehot_product(local_ids, row_total, token_rows):
    columns = lax.broadcasted_iota(jnp.int32, (1, row_total), 1)
    onehot = (local_ids[:, None] == columns).astype(jnp.bfloat16)
    return lax.dot_general(
        onehot, token_rows, (((0,), (0,)), ((), ())), preferred_element_type=jnp.float32
    )


def window_gradient(window_ids, window_rows, own_start, row_count, vocab_rows):
    width = window_rows.shape[2]
    head_rows, head_ids = shifted(
        (window_rows[:, :TOK_EDGE], window_ids[:, :TOK_EDGE]), "vocab", -1
    )
    tail_rows, tail_ids = shifted(
        (window_rows[:, -TOK_EDGE:], window_ids[:, -TOK_EDGE:]), "vocab", 1
    )
    all_rows = jnp.concatenate([tail_rows, window_rows, head_rows], axis=1)
    all_ids = jnp.concatenate([tail_ids, window_ids, head_ids], axis=1)
    local_ids = jnp.mod(all_ids.reshape(-1) - own_start, vocab_rows)
    gradient = onehot_product(local_ids, row_count, all_rows.reshape(-1, width))
    return gradient


def body(embed_table, token_ids, grad_rows):
    row_count = embed_table.shape[0]
    width = embed_table.shape[1]
    vocab_rows = row_count * lax.axis_size("vocab")
    own_start = lax.axis_index("vocab") * row_count
    gradient = window_gradient(token_ids, grad_rows, own_start, row_count, vocab_rows)
    shared = lax.psum_scatter(gradient, "dp", scatter_dimension=1, tiled=True)
    sum_squares = lax.psum(jnp.sum(shared * shared), ("vocab", "dp"))
    element_count = vocab_rows * width
    grad_rms = jnp.sqrt(sum_squares / element_count)
    clip_scale = 1.0 / jnp.maximum(1.0, grad_rms / norm_limit)
    half_width = shared.shape[1]
    own_columns = lax.dynamic_slice_in_dim(
        embed_table, lax.axis_index("dp") * half_width, half_width, 1
    )
    updated = (own_columns.astype(jnp.float32) - step_rate * clip_scale * shared).astype(
        jnp.bfloat16
    )
    return (updated, jnp.reshape(grad_rms, (1,)))


def solution(mesh):
    in_specs = (P("vocab", None), P("dp", "vocab"), P("dp", "vocab", None))
    out_specs = (P("vocab", "dp"), P())
    return jax.shard_map(body, mesh=mesh, in_specs=in_specs, out_specs=out_specs, check_vma=False)
```

profile of v0, /device:TPU:0, one launch (start us, length us, event | category | flops | bytes accessed | tf_op | source)
XLA Modules:
  0.0 166.0 jit_solution(1703187708787858095)
XLA Ops:
  7.2 0.0 reduce-scatter.2.cloned.1.call-start
  7.2 1.7 %fusion.9 = (bf16[1,128,4096]{2,1,0:T(8,128)(2,1)S(1)}, bf16[1,128,4096]{2,1,0:T(8,128)(2,1)S(1)}) fusion(bf16[1,1024,4096]{2,1,0:T(8,128)(2,1)} %param.5), kind=kLoop, calls=%fused_computation.17 | loop fusion | bytes 4194304 | tf_op jit(solution)/shard_map/slice | solution.py:33
  8.9 3.0 %collective-permute-start.2 = (bf16[1,128,4096]{2,1,0:T(8,128)(2,1)S(1)}, bf16[1,128,4096]{2,1,0:T(8,128)(2,1)S(1)}, u32[]{:S(2)}, u32[]{:S(2)}) collective-permute-start(bf16[1,128,4096]{2,1,0:T(8,128)(2,1)S(1)} %get-tuple-element.2), channel_id=1, source_target_pairs={{30,0},{0,2},{2,4},{4,6},{6,8},{8,10},{10,12},{12,14},{14,16},{16,... | collective-permute-start | bytes 3145736 | tf_op jit(solution)/shard_map/ppermute | solution.py:16
  11.9 4.1 %collective-permute-start.3 = (bf16[1,128,4096]{2,1,0:T(8,128)(2,1)S(1)}, bf16[1,128,4096]{2,1,0:T(8,128)(2,1)}, u32[]{:S(2)}, u32[]{:S(2)}) collective-permute-start(bf16[1,128,4096]{2,1,0:T(8,128)(2,1)S(1)} %get-tuple-element.3), channel_id=1, source_target_pairs={{2,0},{4,2},{6,4},{8,6},{10,8},{12,10},{14,12},{16,14},{18,16},{20... | collective-permute-start | bytes 3145736 | tf_op jit(solution)/shard_map/ppermute | solution.py:16
  16.0 0.7 fusion.10
  16.6 0.0 collective-permute-start
  16.6 5.6 %collective-permute-start.1 = (s32[1,128]{1,0:T(1,128)S(1)}, s32[1,128]{1,0:T(1,128)S(1)}, u32[]{:S(2)}, u32[]{:S(2)}) collective-permute-start(s32[1,128]{1,0:T(1,128)S(1)} %get-tuple-element.5), channel_id=1, source_target_pairs={{2,0},{4,2},{6,4},{8,6},{10,8},{12,10},{14,12},{16,14},{18,16},{20... | collective-permute-start | bytes 1544 | tf_op jit(solution)/shard_map/ppermute | solution.py:16
  22.3 34.6 %collective-permute-done = s32[1,128]{1,0:T(1,128)S(1)} collective-permute-done((s32[1,128]{1,0:T(1,128)S(1)}, s32[1,128]{1,0:T(1,128)S(1)}, u32[]{:S(2)}, u32[]{:S(2)}) %collective-permute-start) | collective-permute-done | bytes 544 | tf_op jit(solution)/shard_map/ppermute | solution.py:16
  56.9 2.0 %collective-permute-done.1 = s32[1,128]{1,0:T(1,128)S(1)} collective-permute-done((s32[1,128]{1,0:T(1,128)S(1)}, s32[1,128]{1,0:T(1,128)S(1)}, u32[]{:S(2)}, u32[]{:S(2)}) %collective-permute-start.1) | collective-permute-done | bytes 544 | tf_op jit(solution)/shard_map/ppermute | solution.py:16
  58.9 0.7 fusion.7
  59.6 0.0 collective-permute-done.2
  59.6 0.0 collective-permute-done.3
  59.6 17.0 %fusion = f32[1024,4096]{1,0:T(8,128)} fusion(bf16[1,128,4096]{2,1,0:T(8,128)(2,1)} %collective-permute-done.3, bf16[1,1024,4096]{2,1,0:T(8,128)(2,1)} %param.5, bf16[1,128,4096]{2,1,0:T(8,128)(2,1)S(1)} %collective-permute-done.2, s32[1280]{0:T(1024)S(1)} %add_select_fusion), kind=kOutput, calls=%fused_computation.1 | convolution fusion | flops 10770186240 | bytes 27268096 | tf_op jit(solution)/shard_map/dot_general | solution.py:22
  76.6 0.0 reduce-scatter.2.cloned.1.call-update
  76.7 25.4 %reduce-scatter.2.cloned.1.call-done = f32[1024,2048]{1,0:T(8,128)} async-done(((f32[1024,4096]{1,0:T(8,128)}), f32[1024,2048]{1,0:T(8,128)}) %reduce-scatter.2.cloned.1.call-update) | async-done | bytes 8388624 | tf_op jit(solution)/shard_map/reduce_scatter | solution.py:48
  102.1 6.1 %multiply_reduce_fusion = f32[]{:T(128)} fusion(f32[1024,2048]{1,0:T(8,128)} %reduce-scatter.2.cloned.1.call-done), kind=kLoop, calls=%fused_computation.7 | loop fusion | flops 4194303 | bytes 8388612 | tf_op jit(solution)/shard_map/reduce_sum | solution.py:49
  108.2 40.8 %psum.7 = f32[]{:T(128)} all-reduce(f32[]{:T(128)} %multiply_reduce_fusion), channel_id=1, replica_groups=mesh['vocab'=16,'dp'=2] {'vocab','dp'}, use_global_device_ids=true, to_apply=%region_2.3 | all-reduce | flops 1 | bytes 8 | tf_op jit(solution)/shard_map/psum | solution.py:49
  149.7 8.3 %subtract_convert_fusion = bf16[1024,2048]{1,0:T(8,128)(2,1)} fusion(f32[1024,2048]{1,0:T(8,128)} %reduce-scatter.2.cloned.1.call-done, f32[]{:T(128)S(6)} %mul_shard_map.3, bf16[1024,4096]{1,0:T(8,128)(2,1)} %param.3, s32[]{:T(128)S(6)} %select_n.14), kind=kLoop, calls=%fused_computation.6 | loop fusion | flops 8388608 | bytes 16777224 | tf_op jit(solution)/shard_map/convert_element_type | solution.py:57
  (1 shorter events, 0.0 us)
Async XLA Ops:
  7.2 94.9 %reduce-scatter.2.cloned.1.call-start = ((), (), s32[]{:S(2)}) async-start(), calls=%async_computation.1 | async-start | bytes 25165824 | tf_op jit(solution)/shard_map/reduce_scatter | solution.py:48
  8.9 50.7 %collective-permute-start.2 = (bf16[1,128,4096]{2,1,0:T(8,128)(2,1)S(1)}, bf16[1,128,4096]{2,1,0:T(8,128)(2,1)S(1)}, u32[]{:S(2)}, u32[]{:S(2)}) collective-permute-start(bf16[1,128,4096]{2,1,0:T(8,128)(2,1)S(1)} %get-tuple-element.2), channel_id=1, source_target_pairs={{30,0},{0,2},{2,4},{4,6},{6,8},{8,10},{10,12},{12,14},{14,16},{16,... | collective-permute-start | bytes 3145736 | tf_op jit(solution)/shard_map/ppermute | solution.py:16
  11.9 47.7 %collective-permute-start.3 = (bf16[1,128,4096]{2,1,0:T(8,128)(2,1)S(1)}, bf16[1,128,4096]{2,1,0:T(8,128)(2,1)}, u32[]{:S(2)}, u32[]{:S(2)}) collective-permute-start(bf16[1,128,4096]{2,1,0:T(8,128)(2,1)S(1)} %get-tuple-element.3), channel_id=1, source_target_pairs={{2,0},{4,2},{6,4},{8,6},{10,8},{12,10},{14,12},{16,14},{18,16},{20... | collective-permute-start | bytes 3145736 | tf_op jit(solution)/shard_map/ppermute | solution.py:16
  16.6 40.2 %collective-permute-start = (s32[1,128]{1,0:T(1,128)S(1)}, s32[1,128]{1,0:T(1,128)S(1)}, u32[]{:S(2)}, u32[]{:S(2)}) collective-permute-start(s32[1,128]{1,0:T(1,128)S(1)} %get-tuple-element.4), channel_id=1, source_target_pairs={{30,0},{0,2},{2,4},{4,6},{6,8},{8,10},{10,12},{12,14},{14,16},{16,... | collective-permute-start | bytes 1544 | tf_op jit(solution)/shard_map/ppermute | solution.py:16
  16.6 42.2 %collective-permute-start.1 = (s32[1,128]{1,0:T(1,128)S(1)}, s32[1,128]{1,0:T(1,128)S(1)}, u32[]{:S(2)}, u32[]{:S(2)}) collective-permute-start(s32[1,128]{1,0:T(1,128)S(1)} %get-tuple-element.5), channel_id=1, source_target_pairs={{2,0},{4,2},{6,4},{8,6},{10,8},{12,10},{14,12},{16,14},{18,16},{20... | collective-permute-start | bytes 1544 | tf_op jit(solution)/shard_map/ppermute | solution.py:16
Sparse Core Ops, SparseCore 0:
  76.8 25.2 reduce-scatter.1
where the time goes:
time: 166 us
  waiting for transfers between devices  62 us (37%)
  blocking collectives  40.8 us (25%)
  matrix products  17 us (10%)
  between operations  15.9 us (10%)
  other arithmetic  15.2 us (9%)
  starting transfers between devices  12.7 us (8%)
  local copies, waits for them, and re-layouts  2.35 us (1%)
    psum x1, blocking collectives, body(): sum_squares = lax.psum(jnp.sum(shared * shared), ('vocab', 'dp'))  40.8 us
    ppermute x4, waiting for transfers between devices, shifted(): return lax.ppermute(block, axis, route)  36.6 us
    reduce_scatter x1, waiting for transfers between devices, body(): shared = lax.psum_scatter(gradient, 'dp', scatter_dimension=1, tiled=True)  25.4 us
    dot_general x1, matrix products, onehot_product(): lax.dot_general(onehot, token_rows, (((0,), (0,)), ((), ())), preferred_e...  17 us
    ppermute x4, starting transfers between devices, shifted(): return lax.ppermute(block, axis, route)  12.7 us
    convert_element_type x1, other arithmetic, body(): (own_columns.astype(jnp.float32) - step_rate * clip_scale * shared).astyp...  8.33 us
    reduce_sum x1, other arithmetic, body(): sum_squares = lax.psum(jnp.sum(shared * shared), ('vocab', 'dp'))  6.14 us
  transfers between devices with their start and end apart: 5, of which 3 were waited for; matrix products, arithmetic and copies ran while one was open for 1% of the time, Pallas kernels for 0%

commit v1 on v0

v1 whole, which is shorter than its diff:
```python
import functools

import jax
import jax.numpy as jnp
from jax import lax
from jax.experimental import pallas as pl
from jax.experimental.pallas import tpu as pltpu
from jax.sharding import PartitionSpec as P

MESH = pl.DeviceIdType.MESH
TOK_EDGE = 128
EDGE = 256
COLS = 512
STORE_ROWS = 128

step_rate = 0.5
norm_limit = 1.0


def kernel(sizes, table_ref, ids_ref, grad_ref, out_ref, rms_ref,
           toks, halo, table, grad, outbuf, mate_ids, halo_ids, square, sums,
           own_sem, table_sem, mate_sem, mate_id_sem, halo_send, halo_recv,
           halo_id_send, halo_id_recv, sum_send, sum_recv, out_sem):
    n_vocab, n_dp = sizes
    rows, width = table_ref.shape
    tokens = ids_ref.shape[1]
    half = width // n_dp
    n = n_vocab * n_dp
    chunks = half // COLS
    blocks = rows // EDGE
    v = lax.axis_index("vocab")
    p = lax.axis_index("dp")
    me = v * n_dp + p
    mate = 1 - p
    below = lax.rem(v + n_vocab - 1, n_vocab)
    above = lax.rem(v + 1, n_vocab)

    def columns(core, chunk):
        return pl.ds(pl.multiple_of(core * half + chunk * COLS, COLS), COLS)

    def place(index):
        return {"vocab": lax.div(index, n_dp), "dp": lax.rem(index, n_dp)}

    own_half = pl.ds(pl.multiple_of(p * half, half), half)
    own_copy = pltpu.make_async_copy(
        grad_ref.at[0, :, own_half], toks.at[pl.ds(0, tokens), :], own_sem
    )
    own_copy.start()
    table_copy = pltpu.make_async_copy(table_ref.at[:, own_half], table, table_sem)

    barrier = pltpu.get_barrier_semaphore()

    @pl.loop(1, n)
    def _(i):
        pl.semaphore_signal(
            barrier, inc=1, device_id=place(lax.rem(me + i, n)), device_id_type=MESH
        )

    pl.semaphore_wait(barrier, n - 1)

    def remote(src, dst, send, recv, device):
        return pltpu.make_async_remote_copy(
            src_ref=src, dst_ref=dst, send_sem=send, recv_sem=recv,
            device_id=device, device_id_type=MESH,
        )

    sent = []
    mate_id_copy = remote(
        ids_ref, mate_ids, mate_id_sem.at[0], mate_id_sem.at[1], {"vocab": v, "dp": mate}
    )
    mate_id_copy.start()
    sides = ((0, 0, below), (1, tokens - TOK_EDGE, above))
    for side, first, target in sides:
        for core in range(n_dp):
            copy = remote(
                ids_ref.at[:, pl.ds(first, TOK_EDGE)], halo_ids.at[side, p],
                halo_id_send.at[side, core], halo_id_recv.at[side, p],
                {"vocab": target, "dp": core},
            )
            copy.start()
            sent.append(copy)
    mate_copies = []
    for chunk in range(chunks):
        for side, first, target in sides:
            for core in range(n_dp):
                copy = remote(
                    grad_ref.at[0, pl.ds(first, TOK_EDGE), columns(core, chunk)],
                    halo.at[side, p, :, pl.ds(chunk * COLS, COLS)],
                    halo_send.at[side, core, chunk], halo_recv.at[side, p, chunk],
                    {"vocab": target, "dp": core},
                )
                copy.start()
                sent.append(copy)
        copy = remote(
            grad_ref.at[0, :, columns(mate, chunk)],
            toks.at[pl.ds(tokens, tokens), pl.ds(chunk * COLS, COLS)],
            mate_sem.at[0, chunk], mate_sem.at[1, chunk], {"vocab": v, "dp": mate},
        )
        copy.start()
        mate_copies.append(copy)
    table_copy.start()

    own_start = v * rows

    def local(ids):
        shifted = ids - own_start
        return jnp.where(shifted < 0, shifted + n_vocab * rows, shifted)

    def onehot(ids, base, count):
        index = lax.broadcasted_iota(jnp.int32, (count, ids.shape[1]), 0) + base
        return jnp.where(ids == index, 1.0, 0.0).astype(jnp.bfloat16)

    def add_squares(values):
        lanes = values * values
        lanes = jnp.sum(lanes.reshape(EDGE // 8, 8, COLS), axis=0)
        square[...] += lanes

    square[...] = jnp.zeros_like(square)
    own_copy.wait()
    mate_id_copy.wait()
    for copy in mate_copies:
        copy.wait()
    window_ids = local(jnp.concatenate([ids_ref[...], mate_ids[...]], axis=1))
    for block in range(blocks):
        picked = onehot(window_ids, block * EDGE, EDGE)

        @pl.loop(0, chunks)
        def _(chunk):
            here = pl.ds(pl.multiple_of(chunk * COLS, COLS), COLS)
            part = jnp.dot(picked, toks[:, here], preferred_element_type=jnp.float32)
            grad[pl.ds(block * EDGE, EDGE), here] = part
            if 0 < block < blocks - 1:
                add_squares(part)

    table_copy.wait()
    halo_pick = []
    for side in range(2):
        for core in range(n_dp):
            remote(
                ids_ref.at[:, pl.ds(0, TOK_EDGE)], halo_ids.at[side, core],
                halo_id_send.at[side, core], halo_id_recv.at[side, core],
                {"vocab": above, "dp": core},
            ).wait_recv()
        ids = local(jnp.concatenate([halo_ids[side, core] for core in range(n_dp)], axis=1))
        base = (rows - EDGE) if side == 0 else 0
        halo_pick.append((base, onehot(ids, base, EDGE)))
    for chunk in range(chunks):
        here = pl.ds(chunk * COLS, COLS)
        for side in range(2):
            for core in range(n_dp):
                remote(
                    grad_ref.at[0, pl.ds(0, TOK_EDGE), pl.ds(0, COLS)],
                    halo.at[side, core, :, here],
                    halo_send.at[side, core, chunk], halo_recv.at[side, core, chunk],
                    {"vocab": above, "dp": core},
                ).wait_recv()
            base, pick = halo_pick[side]
            part = jnp.dot(
                pick, halo[side, :, :, here].reshape(n_dp * TOK_EDGE, COLS),
                preferred_element_type=jnp.float32,
            )
            total = grad[pl.ds(base, EDGE), here] + part
            grad[pl.ds(base, EDGE), here] = total
            add_squares(total)

    lanes = jnp.sum(square[...], axis=0, keepdims=True)
    lanes = functools.reduce(
        jnp.add, [lanes[:, k * 128:(k + 1) * 128] for k in range(COLS // 128)]
    )
    sums[me] = lanes

    def sum_copy(i, source, target):
        return remote(
            sums.at[source], sums.at[source], sum_send.at[i], sum_recv.at[source], place(target)
        )

    @pl.loop(1, n)
    def _(i):
        sum_copy(i, me, lax.rem(me + i, n)).start()

    for copy in sent:
        copy.wait_send()

    @pl.loop(1, n)
    def _(i):
        source = lax.rem(me + i, n)
        sum_copy(i, source, source).wait_recv()

    total = jnp.sum(jnp.sum(sums[...], axis=0), axis=1, keepdims=True)
    rms = jnp.sqrt(total / (n_vocab * rows * width))
    clip_scale = 1.0 / jnp.maximum(1.0, rms / norm_limit)
    rms_ref[0] = rms[0, 0]
    rate = step_rate * clip_scale

    stores = []
    for block in range(rows // STORE_ROWS):
        here = pl.ds(block * STORE_ROWS, STORE_ROWS)
        moved = table[here, :].astype(jnp.float32) - rate * grad[here, :]
        outbuf[here, :] = moved.astype(jnp.bfloat16)
        copy = pltpu.make_async_copy(outbuf.at[here, :], out_ref.at[here, :], out_sem.at[block])
        copy.start()
        stores.append(copy)

    @pl.loop(1, n)
    def _(i):
        sum_copy(i, me, lax.rem(me + i, n)).wait_send()

    for copy in stores:
        copy.wait()


def solution(mesh):
    n_vocab, n_dp = mesh.shape["vocab"], mesh.shape["dp"]
    n = n_vocab * n_dp

    def body(embed_table, token_ids, grad_rows):
        rows, width = embed_table.shape
        tokens = token_ids.shape[1]
        half = width // n_dp
        chunks = half // COLS
        anywhere = pl.BlockSpec(memory_space=pl.ANY)
        updated, grad_rms = pl.pallas_call(
            functools.partial(kernel, (n_vocab, n_dp)),
            name="clipped_update",
            out_shape=(
                jax.ShapeDtypeStruct((rows, half), jnp.bfloat16),
                jax.ShapeDtypeStruct((1,), jnp.float32),
            ),
            in_specs=[anywhere, pl.BlockSpec(memory_space=pltpu.VMEM), anywhere],
            out_specs=(anywhere, pl.BlockSpec(memory_space=pltpu.SMEM)),
            scratch_shapes=[
                pltpu.VMEM((n_dp * tokens, half), jnp.bfloat16),
                pltpu.VMEM((2, n_dp, TOK_EDGE, half), jnp.bfloat16),
                pltpu.VMEM((rows, half), jnp.bfloat16),
                pltpu.VMEM((rows, half), jnp.float32),
                pltpu.VMEM((rows, half), jnp.bfloat16),
                pltpu.VMEM((1, tokens), jnp.int32),
                pltpu.VMEM((2, n_dp, 1, TOK_EDGE), jnp.int32),
                pltpu.VMEM((8, COLS), jnp.float32),
                pltpu.VMEM((n, 1, 128), jnp.float32),
                pltpu.SemaphoreType.DMA,
                pltpu.SemaphoreType.DMA,
                pltpu.SemaphoreType.DMA((2, chunks)),
                pltpu.SemaphoreType.DMA((2,)),
                pltpu.SemaphoreType.DMA((2, n_dp, chunks)),
                pltpu.SemaphoreType.DMA((2, n_dp, chunks)),
                pltpu.SemaphoreType.DMA((2, n_dp)),
                pltpu.SemaphoreType.DMA((2, n_dp)),
                pltpu.SemaphoreType.DMA((n,)),
                pltpu.SemaphoreType.DMA((n,)),
                pltpu.SemaphoreType.DMA((rows // STORE_ROWS,)),
            ],
            compiler_params=pltpu.CompilerParams(
                collective_id=0, has_side_effects=True, vmem_limit_bytes=60 * 1024 * 1024
            ),
        )(embed_table, token_ids, grad_rows)
        return updated, grad_rms

    in_specs = (P("vocab", None), P("dp", "vocab"), P("dp", "vocab", None))
    out_specs = (P("vocab", "dp"), P())
    return jax.shard_map(body, mesh=mesh, in_specs=in_specs, out_specs=out_specs, check_vma=False)
```

time: 166 us -> 69.4 us (0.42)
  Pallas kernels: 0 us -> 62 us
  waiting for transfers between devices: 62 us -> 0 us
  blocking collectives: 40.8 us -> 0 us
  matrix products: 17 us -> 0 us
  other arithmetic: 15.2 us -> 0 us
  between operations: 15.9 us -> 2.37 us
  starting transfers between devices: 12.7 us -> 0 us
  local copies, waits for them, and re-layouts: 2.35 us -> 4.79 us
    pallas_call x0 -> x1, Pallas kernels: none -> 62 us  [body(): pl.pallas_call(functools.partial(kernel, (n_vocab, n_dp)), name='clipped_...]
    psum x1 -> x0, blocking collectives: 40.8 us -> none  [body(): sum_squares = lax.psum(jnp.sum(shared * shared), ('vocab', 'dp'))]
    ppermute x4 -> x0, waiting for transfers between devices: 36.6 us -> none  [shifted(): return lax.ppermute(block, axis, route)]
    reduce_scatter x1 -> x0, waiting for transfers between devices: 25.4 us -> none  [body(): shared = lax.psum_scatter(gradient, 'dp', scatter_dimension=1, tiled=True)]
    dot_general x1 -> x0, matrix products: 17 us -> none  [onehot_product(): lax.dot_general(onehot, token_rows, (((0,), (0,)), ((), ())), preferred_e...]
    ppermute x4 -> x0, starting transfers between devices: 12.7 us -> none  [shifted(): return lax.ppermute(block, axis, route)]
    convert_element_type x1 -> x0, other arithmetic: 8.33 us -> none  [body(): (own_columns.astype(jnp.float32) - step_rate * clip_scale * shared).astyp...]
    reduce_sum x1 -> x0, other arithmetic: 6.14 us -> none  [body(): sum_squares = lax.psum(jnp.sum(shared * shared), ('vocab', 'dp'))]
  transfers between devices with their start and end apart: 5 -> 0, of which waited for: 3 -> 0; matrix products, arithmetic and copies ran while one was open for 1% -> 0% of each run, Pallas kernels for 0% -> 0%
where the time goes in v1:
time: 69.4 us; the launch traced here: 69.2 us
  Pallas kernels  62 us (89%)
  local copies, waits for them, and re-layouts  4.79 us (7%)
  between operations  2.37 us (3%)
    pallas_call x1, Pallas kernels, body(): pl.pallas_call(functools.partial(kernel, (n_vocab, n_dp)), name='clipped_...  62 us
    unnamed x1, local copies, waits for them, and re-layouts  4.79 us

profile of v1, /device:TPU:0, one launch (start us, length us, event | category | flops | bytes accessed | tf_op | source)
XLA Modules:
  0.0 69.2 jit_solution(7983016121296518565)
XLA Ops:
  0.6 62.0 %clipped_update.1 = (bf16[1024,2048]{1,0:T(8,128)(2,1)}, f32[1]{0:T(128)}) custom-call(bf16[1024,4096]{1,0:T(8,128)(2,1)} %table_ref.1, s32[1,1024]{1,0:T(1,128)} %ids_ref.1, bf16[1,1024,4096]{2,1,0:T(8,128)(2,1)} %grad_ref.1), custom_call_target="tpu_custom_call" | custom-call | tf_op jit(solution)/shard_map/clipped_update/pallas_call | solution.py:222
  62.6 4.8 %copy.7 = bf16[1024,2048]{1,0:T(8,128)(2,1)} copy(bf16[1024,2048]{1,0:T(8,128)(2,1)} %get-tuple-element.4) | data formatting | bytes 8388608

commit v2 on v1

--- a/solution.py
+++ b/solution.py
@@ -17,10 +17,10 @@
 norm_limit = 1.0
 
 
-def kernel(sizes, table_ref, ids_ref, grad_ref, out_ref, rms_ref,
-           toks, halo, table, grad, outbuf, mate_ids, halo_ids, square, sums,
-           own_sem, table_sem, mate_sem, mate_id_sem, halo_send, halo_recv,
-           halo_id_send, halo_id_recv, sum_send, sum_recv, out_sem):
+def kernel(sizes, table_ref, ids_ref, grad_ref, grad, table, norm_ref,
+           toks, halo, own_ids, mate_ids, halo_ids, square, sums,
+           own_sem, own_id_sem, table_sem, mate_sem, mate_id_sem, halo_send, halo_recv,
+           halo_id_send, halo_id_recv, sum_send, sum_recv):
     n_vocab, n_dp = sizes
     rows, width = table_ref.shape
     tokens = ids_ref.shape[1]
@@ -46,6 +46,8 @@
         grad_ref.at[0, :, own_half], toks.at[pl.ds(0, tokens), :], own_sem
     )
     own_copy.start()
+    own_id_copy = pltpu.make_async_copy(ids_ref, own_ids, own_id_sem)
+    own_id_copy.start()
     table_copy = pltpu.make_async_copy(table_ref.at[:, own_half], table, table_sem)
 
     barrier = pltpu.get_barrier_semaphore()
@@ -117,10 +119,11 @@
 
     square[...] = jnp.zeros_like(square)
     own_copy.wait()
+    own_id_copy.wait()
     mate_id_copy.wait()
     for copy in mate_copies:
         copy.wait()
-    window_ids = local(jnp.concatenate([ids_ref[...], mate_ids[...]], axis=1))
+    window_ids = local(jnp.concatenate([own_ids[...], mate_ids[...]], axis=1))
     for block in range(blocks):
         picked = onehot(window_ids, block * EDGE, EDGE)
 
@@ -189,22 +192,25 @@
     total = jnp.sum(jnp.sum(sums[...], axis=0), axis=1, keepdims=True)
     rms = jnp.sqrt(total / (n_vocab * rows * width))
     clip_scale = 1.0 / jnp.maximum(1.0, rms / norm_limit)
-    rms_ref[0] = rms[0, 0]
-    rate = step_rate * clip_scale
-
+    norm_ref[0:1, :] = jnp.broadcast_to(step_rate * clip_scale, (1, 128))
+    norm_ref[1:2, :] = jnp.broadcast_to(rms, (1, 128))
+
+    @pl.loop(1, n)
+    def _(i):
+        sum_copy(i, me, lax.rem(me + i, n)).wait_send()
+
+
+def update(grad, table, norm_ref, out_ref, rms_ref, outbuf, out_sem):
+    rate = norm_ref[0:1, 0:1]
     stores = []
-    for block in range(rows // STORE_ROWS):
+    for block in range(grad.shape[0] // STORE_ROWS):
         here = pl.ds(block * STORE_ROWS, STORE_ROWS)
         moved = table[here, :].astype(jnp.float32) - rate * grad[here, :]
         outbuf[here, :] = moved.astype(jnp.bfloat16)
         copy = pltpu.make_async_copy(outbuf.at[here, :], out_ref.at[here, :], out_sem.at[block])
         copy.start()
         stores.append(copy)
-
-    @pl.loop(1, n)
-    def _(i):
-        sum_copy(i, me, lax.rem(me + i, n)).wait_send()
-
+    rms_ref[0] = norm_ref[1, 0]
     for copy in stores:
         copy.wait()
 
@@ -218,26 +224,27 @@
         tokens = token_ids.shape[1]
         half = width // n_dp
         chunks = half // COLS
-        anywhere = pl.BlockSpec(memory_space=pl.ANY)
-        updated, grad_rms = pl.pallas_call(
+        in_vmem = pl.BlockSpec(memory_space=pltpu.VMEM)
+        in_hbm = pl.BlockSpec(memory_space=pltpu.HBM)
+        grad, table, norm = pl.pallas_call(
             functools.partial(kernel, (n_vocab, n_dp)),
             name="clipped_update",
             out_shape=(
+                jax.ShapeDtypeStruct((rows, half), jnp.float32),
                 jax.ShapeDtypeStruct((rows, half), jnp.bfloat16),
-                jax.ShapeDtypeStruct((1,), jnp.float32),
+                jax.ShapeDtypeStruct((8, 128), jnp.float32),
             ),
-            in_specs=[anywhere, pl.BlockSpec(memory_space=pltpu.VMEM), anywhere],
-            out_specs=(anywhere, pl.BlockSpec(memory_space=pltpu.SMEM)),
+            in_specs=[in_hbm, in_hbm, in_hbm],
+            out_specs=(in_vmem, in_vmem, in_vmem),
             scratch_shapes=[
                 pltpu.VMEM((n_dp * tokens, half), jnp.bfloat16),
                 pltpu.VMEM((2, n_dp, TOK_EDGE, half), jnp.bfloat16),
-                pltpu.VMEM((rows, half), jnp.bfloat16),
-                pltpu.VMEM((rows, half), jnp.float32),
-                pltpu.VMEM((rows, half), jnp.bfloat16),
+                pltpu.VMEM((1, tokens), jnp.int32),
                 pltpu.VMEM((1, tokens), jnp.int32),
                 pltpu.VMEM((2, n_dp, 1, TOK_EDGE), jnp.int32),
                 pltpu.VMEM((8, COLS), jnp.float32),
                 pltpu.VMEM((n, 1, 128), jnp.float32),
+                pltpu.SemaphoreType.DMA,
                 pltpu.SemaphoreType.DMA,
                 pltpu.SemaphoreType.DMA,
                 pltpu.SemaphoreType.DMA((2, chunks)),
@@ -248,12 +255,26 @@
                 pltpu.SemaphoreType.DMA((2, n_dp)),
                 pltpu.SemaphoreType.DMA((n,)),
                 pltpu.SemaphoreType.DMA((n,)),
+            ],
+            compiler_params=pltpu.CompilerParams(
+                collective_id=0, has_side_effects=True, vmem_limit_bytes=38 * 1024 * 1024
+            ),
+        )(*(pltpu.with_memory_space_constraint(x, pltpu.HBM) for x in (embed_table, token_ids, grad_rows)))
+        updated, grad_rms = pl.pallas_call(
+            update,
+            name="clipped_step",
+            out_shape=(
+                jax.ShapeDtypeStruct((rows, half), jnp.bfloat16),
+                jax.ShapeDtypeStruct((1,), jnp.float32),
+            ),
+            in_specs=[in_vmem, in_vmem, in_vmem],
+            out_specs=(in_hbm, pl.BlockSpec(memory_space=pltpu.SMEM)),
+            scratch_shapes=[
+                pltpu.VMEM((rows, half), jnp.bfloat16),
                 pltpu.SemaphoreType.DMA((rows // STORE_ROWS,)),
             ],
-            compiler_params=pltpu.CompilerParams(
-                collective_id=0, has_side_effects=True, vmem_limit_bytes=60 * 1024 * 1024
-            ),
-        )(embed_table, token_ids, grad_rows)
+            compiler_params=pltpu.CompilerParams(vmem_limit_bytes=24 * 1024 * 1024),
+        )(grad, table, norm)
         return updated, grad_rms
 
     in_specs = (P("vocab", None), P("dp", "vocab"), P("dp", "vocab", None))

time: 69.4 us -> 62.6 us (0.902)
  local copies, waits for them, and re-layouts: 4.79 us -> 0 us
  between operations: 2.37 us -> 0.64 us
    unnamed x1 -> x0, local copies, waits for them, and re-layouts: 4.79 us -> none
    pallas_call x1, Pallas kernels: 62 us -> 58.5 us  [body(): pl.pallas_call(functools.partial(kernel, (n_vocab, n_dp)), name='clipped_...]
    pallas_call x0 -> x1, Pallas kernels: none -> 3.36 us  [body(): pl.pallas_call(update, name='clipped_step', out_shape=(jax.ShapeDtypeStru...]
where the time goes in v2:
time: 62.6 us; the launch traced here: 62.5 us
  Pallas kernels  61.8 us (99%)
  between operations  0.64 us (1%)
    pallas_call x1, Pallas kernels, body(): pl.pallas_call(functools.partial(kernel, (n_vocab, n_dp)), name='clipped_...  58.5 us
    pallas_call x1, Pallas kernels, body(): pl.pallas_call(update, name='clipped_step', out_shape=(jax.ShapeDtypeStru...  3.36 us

profile of v2, /device:TPU:0, one launch (start us, length us, event | category | flops | bytes accessed | tf_op | source)
XLA Modules:
  0.0 62.5 jit_solution(6524305016125587966)
XLA Ops:
  0.6 58.5 %clipped_update.1 = (f32[1024,2048]{1,0:T(8,128)S(1)}, bf16[1024,2048]{1,0:T(8,128)(2,1)S(1)}, f32[8,128]{1,0:T(8,128)S(1)}) custom-call(bf16[1024,4096]{1,0:T(8,128)(2,1)} %table_ref.1, s32[1,1024]{1,0:T(1,128)} %ids_ref.1, bf16[1,1024,4096]{2,1,0:T(8,128)(2,1)} %grad_ref.1), custom_call_target="tpu_custom_call" | custom-call | tf_op jit(solution)/shard_map/clipped_update/pallas_call | solution.py:229
  59.1 3.4 %clipped_step.1 = (bf16[1024,2048]{1,0:T(8,128)(2,1)}, f32[1]{0:T(128)}) custom-call(f32[1024,2048]{1,0:T(8,128)S(1)} %get-tuple-element.5.grad, bf16[1024,2048]{1,0:T(8,128)(2,1)S(1)} %get-tuple-element.6.table, f32[8,128]{1,0:T(8,128)S(1)} %get-tuple-element.7.norm_ref), custom_call_target="tpu_custom_call" | custom-call | tf_op jit(solution)/shard_map/clipped_step/pallas_call | solution.py:263

commit v3 on v2

--- a/solution.py
+++ b/solution.py
@@ -20,7 +20,7 @@
 def kernel(sizes, table_ref, ids_ref, grad_ref, grad, table, norm_ref,
            toks, halo, own_ids, mate_ids, halo_ids, square, sums,
            own_sem, own_id_sem, table_sem, mate_sem, mate_id_sem, halo_send, halo_recv,
-           halo_id_send, halo_id_recv, sum_send, sum_recv):
+           halo_id_send, halo_id_recv, sum_send, sum_recv, known_sem):
     n_vocab, n_dp = sizes
     rows, width = table_ref.shape
     tokens = ids_ref.shape[1]
@@ -38,8 +38,9 @@
     def columns(core, chunk):
         return pl.ds(pl.multiple_of(core * half + chunk * COLS, COLS), COLS)
 
-    def place(index):
-        return {"vocab": lax.div(index, n_dp), "dp": lax.rem(index, n_dp)}
+    def around(distance):
+        ahead = v + distance
+        return jnp.where(ahead >= n_vocab, ahead - n_vocab, ahead)
 
     own_half = pl.ds(pl.multiple_of(p * half, half), half)
     own_copy = pltpu.make_async_copy(
@@ -52,13 +53,12 @@
 
     barrier = pltpu.get_barrier_semaphore()
 
-    @pl.loop(1, n)
-    def _(i):
+    greeted = [(v, mate)] + [(w, core) for w in (below, above) for core in range(n_dp)]
+    for w, core in greeted:
         pl.semaphore_signal(
-            barrier, inc=1, device_id=place(lax.rem(me + i, n)), device_id_type=MESH
+            barrier, inc=1, device_id={"vocab": w, "dp": core}, device_id_type=MESH
         )
-
-    pl.semaphore_wait(barrier, n - 1)
+    pl.semaphore_wait(barrier, len(greeted))
 
     def remote(src, dst, send, recv, device):
         return pltpu.make_async_remote_copy(
@@ -123,8 +123,21 @@
     mate_id_copy.wait()
     for copy in mate_copies:
         copy.wait()
+    rounds = []
+    while 2 ** len(rounds) < n_vocab // 2:
+        rounds.append(2 ** len(rounds))
+
+    def tell(k):
+        for distance in (rounds[k], n_vocab - rounds[k]):
+            pl.semaphore_signal(
+                known_sem.at[k], inc=1,
+                device_id={"vocab": around(distance), "dp": p}, device_id_type=MESH,
+            )
+
     window_ids = local(jnp.concatenate([own_ids[...], mate_ids[...]], axis=1))
     for block in range(blocks):
+        if block < len(rounds):
+            tell(block)
         picked = onehot(window_ids, block * EDGE, EDGE)
 
         @pl.loop(0, chunks)
@@ -134,6 +147,13 @@
             grad[pl.ds(block * EDGE, EDGE), here] = part
             if 0 < block < blocks - 1:
                 add_squares(part)
+
+        if block < len(rounds):
+            pl.semaphore_wait(known_sem.at[block], 2)
+
+    for k in range(blocks, len(rounds)):
+        tell(k)
+        pl.semaphore_wait(known_sem.at[k], 2)
 
     table_copy.wait()
     halo_pick = []
@@ -172,22 +192,30 @@
     )
     sums[me] = lanes
 
-    def sum_copy(i, source, target):
+    def sum_copy(source, slot, target):
+        w, core = target
         return remote(
-            sums.at[source], sums.at[source], sum_send.at[i], sum_recv.at[source], place(target)
+            sums.at[source], sums.at[source], sum_send.at[slot], sum_recv.at[source],
+            {"vocab": w, "dp": core},
         )
 
-    @pl.loop(1, n)
-    def _(i):
-        sum_copy(i, me, lax.rem(me + i, n)).start()
+    @pl.loop(1, n_vocab)
+    def _(distance):
+        for core in range(n_dp):
+            sum_copy(me, distance * n_dp + core, (around(distance), core)).start()
+
+    sum_copy(me, 0, (v, mate)).start()
 
     for copy in sent:
         copy.wait_send()
 
-    @pl.loop(1, n)
-    def _(i):
-        source = lax.rem(me + i, n)
-        sum_copy(i, source, source).wait_recv()
+    sum_copy(v * n_dp + mate, 0, (v, mate)).wait_recv()
+
+    @pl.loop(1, n_vocab)
+    def _(distance):
+        w = around(distance)
+        for core in range(n_dp):
+            sum_copy(w * n_dp + core, 0, (w, core)).wait_recv()
 
     total = jnp.sum(jnp.sum(sums[...], axis=0), axis=1, keepdims=True)
     rms = jnp.sqrt(total / (n_vocab * rows * width))
@@ -195,9 +223,12 @@
     norm_ref[0:1, :] = jnp.broadcast_to(step_rate * clip_scale, (1, 128))
     norm_ref[1:2, :] = jnp.broadcast_to(rms, (1, 128))
 
-    @pl.loop(1, n)
-    def _(i):
-        sum_copy(i, me, lax.rem(me + i, n)).wait_send()
+    sum_copy(me, 0, (v, mate)).wait_send()
+
+    @pl.loop(1, n_vocab)
+    def _(distance):
+        for core in range(n_dp):
+            sum_copy(me, distance * n_dp + core, (around(distance), core)).wait_send()
 
 
 def update(grad, table, norm_ref, out_ref, rms_ref, outbuf, out_sem):
@@ -255,6 +286,7 @@
                 pltpu.SemaphoreType.DMA((2, n_dp)),
                 pltpu.SemaphoreType.DMA((n,)),
                 pltpu.SemaphoreType.DMA((n,)),
+                pltpu.SemaphoreType.REGULAR((max(n_vocab.bit_length(), 1),)),
             ],
             compiler_params=pltpu.CompilerParams(
                 collective_id=0, has_side_effects=True, vmem_limit_bytes=38 * 1024 * 1024

time: 62.6 us -> 61.9 us (0.989)
  Pallas kernels: 61.8 us -> 61.1 us
    pallas_call x1, Pallas kernels: 58.5 us -> 57.8 us  [body(): pl.pallas_call(functools.partial(kernel, (n_vocab, n_dp)), name='clipped_...]
where the time goes in v3:
time: 61.9 us; the launch traced here: 61.8 us
  Pallas kernels  61.1 us (99%)
  between operations  0.64 us (1%)
    pallas_call x1, Pallas kernels, body(): pl.pallas_call(functools.partial(kernel, (n_vocab, n_dp)), name='clipped_...  57.8 us
    pallas_call x1, Pallas kernels, body(): pl.pallas_call(update, name='clipped_step', out_shape=(jax.ShapeDtypeStru...  3.36 us

profile of v3, /device:TPU:0, one launch (start us, length us, event | category | flops | bytes accessed | tf_op | source)
XLA Modules:
  0.0 61.8 jit_solution(3238442461747194617)
XLA Ops:
  0.6 57.8 %clipped_update.1 = (f32[1024,2048]{1,0:T(8,128)S(1)}, bf16[1024,2048]{1,0:T(8,128)(2,1)S(1)}, f32[8,128]{1,0:T(8,128)S(1)}) custom-call(bf16[1024,4096]{1,0:T(8,128)(2,1)} %table_ref.1, s32[1,1024]{1,0:T(1,128)} %ids_ref.1, bf16[1,1024,4096]{2,1,0:T(8,128)(2,1)} %grad_ref.1), custom_call_target="tpu_custom_call" | custom-call | tf_op jit(solution)/shard_map/clipped_update/pallas_call | solution.py:260
  58.4 3.4 %clipped_step.1 = (bf16[1024,2048]{1,0:T(8,128)(2,1)}, f32[1]{0:T(128)}) custom-call(f32[1024,2048]{1,0:T(8,128)S(1)} %get-tuple-element.5.grad, bf16[1024,2048]{1,0:T(8,128)(2,1)S(1)} %get-tuple-element.6.table, f32[8,128]{1,0:T(8,128)S(1)} %get-tuple-element.7.norm_ref), custom_call_target="tpu_custom_call" | custom-call | tf_op jit(solution)/shard_map/clipped_step/pallas_call | solution.py:295

commit v4 on v3

--- a/solution.py
+++ b/solution.py
@@ -11,7 +11,7 @@
 TOK_EDGE = 128
 EDGE = 256
 COLS = 512
-STORE_ROWS = 128
+STORE_ROWS = 64
 
 step_rate = 0.5
 norm_limit = 1.0
@@ -231,7 +231,10 @@
             sum_copy(me, distance * n_dp + core, (around(distance), core)).wait_send()
 
 
-def update(grad, table, norm_ref, out_ref, rms_ref, outbuf, out_sem):
+def update(grad, table, norm_ref, out_ref, rms_ref, outbuf, rms_held, out_sem, rms_sem):
+    rms_held[0] = norm_ref[1, 0]
+    rms_copy = pltpu.make_async_copy(rms_held, rms_ref, rms_sem)
+    rms_copy.start()
     rate = norm_ref[0:1, 0:1]
     stores = []
     for block in range(grad.shape[0] // STORE_ROWS):
@@ -241,9 +244,9 @@
         copy = pltpu.make_async_copy(outbuf.at[here, :], out_ref.at[here, :], out_sem.at[block])
         copy.start()
         stores.append(copy)
-    rms_ref[0] = norm_ref[1, 0]
     for copy in stores:
         copy.wait()
+    rms_copy.wait()
 
 
 def solution(mesh):
@@ -300,10 +303,12 @@
                 jax.ShapeDtypeStruct((1,), jnp.float32),
             ),
             in_specs=[in_vmem, in_vmem, in_vmem],
-            out_specs=(in_hbm, pl.BlockSpec(memory_space=pltpu.SMEM)),
+            out_specs=(in_hbm, in_hbm),
             scratch_shapes=[
                 pltpu.VMEM((rows, half), jnp.bfloat16),
+                pltpu.SMEM((1,), jnp.float32),
                 pltpu.SemaphoreType.DMA((rows // STORE_ROWS,)),
+                pltpu.SemaphoreType.DMA,
             ],
             compiler_params=pltpu.CompilerParams(vmem_limit_bytes=24 * 1024 * 1024),
         )(grad, table, norm)

time: 61.9 us -> 61.3 us (level)
    pallas_call x1, Pallas kernels: 3.36 us -> 2.69 us  [body(): pl.pallas_call(update, name='clipped_step', out_shape=(jax.ShapeDtypeStru...]
where the time goes in v4:
time: 61.3 us; the launch traced here: 61.1 us
  Pallas kernels  60.5 us (99%)
  between operations  0.64 us (1%)
    pallas_call x1, Pallas kernels, body(): pl.pallas_call(functools.partial(kernel, (n_vocab, n_dp)), name='clipped_...  57.8 us
    pallas_call x1, Pallas kernels, body(): pl.pallas_call(update, name='clipped_step', out_shape=(jax.ShapeDtypeStru...  2.69 us

profile of v4, /device:TPU:0, one launch (start us, length us, event | category | flops | bytes accessed | tf_op | source)
XLA Modules:
  0.0 61.1 jit_solution(3139395482067051504)
XLA Ops:
  0.6 57.8 %clipped_update.1 = (f32[1024,2048]{1,0:T(8,128)S(1)}, bf16[1024,2048]{1,0:T(8,128)(2,1)S(1)}, f32[8,128]{1,0:T(8,128)S(1)}) custom-call(bf16[1024,4096]{1,0:T(8,128)(2,1)} %table_ref.1, s32[1,1024]{1,0:T(1,128)} %ids_ref.1, bf16[1,1024,4096]{2,1,0:T(8,128)(2,1)} %grad_ref.1), custom_call_target="tpu_custom_call" | custom-call | tf_op jit(solution)/shard_map/clipped_update/pallas_call | solution.py:263
  58.4 2.7 %clipped_step.1 = (bf16[1024,2048]{1,0:T(8,128)(2,1)}, f32[1]{0:T(128)}) custom-call(f32[1024,2048]{1,0:T(8,128)S(1)} %get-tuple-element.5.grad, bf16[1024,2048]{1,0:T(8,128)(2,1)S(1)} %get-tuple-element.6.table, f32[8,128]{1,0:T(8,128)S(1)} %get-tuple-element.7.norm_ref), custom_call_target="tpu_custom_call" | custom-call | tf_op jit(solution)/shard_map/clipped_step/pallas_call | solution.py:298
